TPU v7x, 32 devices: a whole 2x2x4 slice. The times are simulated.
32 devices in a mesh: gx: 4 (over y, x), gy: 2 (over core), gz: 4 (over z).
Axes of the slice: x: 2, y: 2, z: 4, core: 2. Of those that a mesh axis runs over, the one named last changes fastest.
Arguments:
- volume: bfloat16 [32, 64, 64, 32], P('gx', 'gy', 'gz'), may hold values from -6 to 6
- conv_in: bfloat16 [3, 3, 3, 32, 32], replicated, may hold values from -0.21875 to 0.21875
- conv_out: bfloat16 [3, 3, 3, 32, 32], replicated, may hold values from -0.21875 to 0.21875
- norm_gain: float32 [256], replicated, may hold values from 0.1 to 1.9
- q_weight: bfloat16 [256, 256], replicated, may hold values from -3 to 3
- kv_weight: bfloat16 [256, 512], replicated, may hold values from -0.375 to 0.375
- out_weight: bfloat16 [256, 256], replicated, may hold values from -0.375 to 0.375
- up_weight: bfloat16 [256, 256], replicated, may hold values from -0.375 to 0.375
Outputs:
- joined_out: bfloat16 [32, 64, 64, 32], P('gx', 'gy', 'gz')
All inputs are finite; a program needn't handle non-finite values.
Results may differ from a plain program's by a relative error of at most 0.012.
The roundings to bfloat16 on the way count: a program that leaves them out, or rounds other values in their place, can miss the bound.
Values may be sent and summed in bfloat16 or wider, within the bound.
No kernel may reach another device: no remote copies, remote signals or barrier semaphores. Data moves between devices by JAX's collectives and lax.ppermute only.
A program may use at most 64 MiB of HBM per device.

v0:
```python
import math
import jax
import jax.numpy as jnp
from jax import lax
from jax.sharding import PartitionSpec as P

HEADS = 8


def with_halo(cells, sides, width):
    for axis, dim in sides:
        count = lax.axis_size(axis)
        ends = count - 1
        head = lax.slice_in_dim(cells, 0, width, axis=dim)
        tail = lax.slice_in_dim(cells, cells.shape[dim] - width, cells.shape[dim], axis=dim)
        cells = jnp.concatenate(
            [
                lax.ppermute(tail, axis, [(i, (i + 1) % count) for i in range(ends)]),
                cells,
                lax.ppermute(head, axis, [((i + 1) % count, i) for i in range(ends)]),
            ],
            axis=dim,
        )
    return cells


def convolve(padded, kernel):
    return lax.conv_general_dilated(
        padded[None],
        kernel,
        (1, 1, 1),
        "VALID",
        dimension_numbers=("NDHWC", "DHWIO", "NDHWC"),
        preferred_element_type=jnp.float32,
    )[0]


def pad_brick(brick):
    return with_halo(brick, (("gx", 0), ("gy", 1), ("gz", 2)), 1)


def tokenize(volume_map):
    extent_x, extent_y, extent_z, channels = volume_map.shape
    grid_cells = volume_map.reshape(
        extent_x // 8, 2, 4, extent_y // 8, 2, 4, extent_z // 8, 2, 4, channels
    ).mean(axis=(2, 5, 8))
    grid_cells = grid_cells.transpose(0, 2, 4, 1, 3, 5, 6)
    return grid_cells.reshape(extent_x // 8 * (extent_y // 8) * (extent_z // 8), 8 * channels)


def spread_cells(token_rows, extent_x, extent_y, extent_z):
    channels = token_rows.shape[1] // 8
    grid_cells = token_rows.reshape(
        extent_x // 8, extent_y // 8, extent_z // 8, 2, 2, 2, channels
    ).transpose(0, 3, 1, 4, 2, 5, 6)
    grid_cells = jnp.broadcast_to(
        grid_cells[:, :, None, :, :, None, :, :, None, :],
        (extent_x // 8, 2, 4, extent_y // 8, 2, 4, extent_z // 8, 2, 4, channels),
    )
    return grid_cells.reshape(extent_x, extent_y, extent_z, channels)


def layer_norm(tokens, norm_gain):
    center = tokens - tokens.mean(axis=1, keepdims=True)
    spread = (center * center).mean(axis=1, keepdims=True)
    return (center * lax.rsqrt(spread + 1e-05) * norm_gain).astype(jnp.bfloat16)


def make_folder(queries, running, shard_piece):
    scaling = queries.shape[-1] ** (-0.5)
    key_count = shard_piece.shape[2]
    block_rows = math.gcd(key_count, 1024)

    def advance(position, state):
        peak_score, denominator, numerator = state
        head_keys = lax.dynamic_slice_in_dim(shard_piece[0], position * block_rows, block_rows, 1)
        head_values = lax.dynamic_slice_in_dim(shard_piece[1], position * block_rows, block_rows, 1)
        scores = (
            jnp.einsum("hqd,hkd->hqk", queries, head_keys, preferred_element_type=jnp.float32)
            * scaling
        )
        new_peak = jnp.maximum(peak_score, scores.max(axis=-1))
        rescale = jnp.exp(peak_score - new_peak)
        weights = jnp.exp(scores - new_peak[..., None])
        denominator = denominator * rescale + weights.sum(axis=-1)
        numerator = numerator * rescale[..., None] + jnp.einsum(
            "hqk,hkd->hqd",
            weights.astype(jnp.bfloat16),
            head_values,
            preferred_element_type=jnp.float32,
        )
        return (new_peak, denominator, numerator)

    return lax.fori_loop(0, key_count // block_rows, advance, running)


def start_state(queries):
    heads_here, query_count, head_size = queries.shape
    return (
        jnp.full((heads_here, query_count), -1e30, jnp.float32),
        jnp.zeros((heads_here, query_count), jnp.float32),
        jnp.zeros((heads_here, query_count, head_size), jnp.float32),
    )


def finish(running):
    return (running[2] / running[1][..., None]).astype(jnp.bfloat16)


def on_device(volume, conv_in, conv_out, norm_gain, q_weight, kv_weight, out_weight, up_weight):
    extent_x, extent_y, extent_z, channels = volume.shape
    encoded = jax.nn.relu(convolve(pad_brick(volume), conv_in)).astype(jnp.bfloat16)
    tokens = tokenize(encoded.astype(jnp.float32))
    normed = layer_norm(tokens, norm_gain)
    queries = jnp.dot(normed, q_weight, preferred_element_type=jnp.float32).astype(jnp.bfloat16)
    key_value = jnp.dot(normed, kv_weight, preferred_element_type=jnp.float32).astype(jnp.bfloat16)
    token_count, width = tokens.shape
    head_size = width // HEADS
    packed = (
        jnp.concatenate([queries, key_value], axis=1)
        .reshape(token_count, 3, HEADS, head_size)
        .transpose(1, 2, 0, 3)
    )
    arranged = lax.all_to_all(packed, "gz", split_axis=1, concat_axis=2, tiled=True)
    head_queries = arranged[0]
    running = make_folder(
        head_queries,
        start_state(head_queries),
        lax.all_gather(arranged[1:], ("gx", "gy"), axis=2, tiled=True),
    )
    returned = lax.all_to_all(finish(running), "gz", split_axis=1, concat_axis=0, tiled=True)
    attended = returned.transpose(1, 0, 2).reshape(token_count, width)
    mixture = (tokens + jnp.dot(attended, out_weight, preferred_element_type=jnp.float32)).astype(
        jnp.bfloat16
    )
    upward = jnp.dot(mixture, up_weight, preferred_element_type=jnp.float32)
    joined = (
        encoded.astype(jnp.float32) + spread_cells(upward, extent_x, extent_y, extent_z)
    ).astype(jnp.bfloat16)
    return convolve(pad_brick(joined), conv_out).astype(jnp.bfloat16)


def solution(mesh):
    placed = (P("gx", "gy", "gz", None), P(), P(), P(), P(), P(), P(), P())
    return jax.shard_map(
        on_device, mesh=mesh, in_specs=placed, out_specs=P("gx", "gy", "gz", None), check_vma=False
    )
```

profile of v0, /device:TPU:0, one launch (start us, length us, event | category | flops | bytes accessed | tf_op | source)
XLA Modules:
  0.0 124.4 jit_solution(1911006101393436707)
XLA Ops:
  0.0 2.0 %copy.101 = bf16[8,32,16,32]{1,3,2,0:T(8,128)(2,1)S(1)} copy(bf16[8,32,16,32]{3,2,1,0:T(8,128)(2,1)} %param.8) | data formatting | bytes 524288 | tf_op args[0]
  2.0 4.9 %collective-permute-start = (bf16[1,32,16,32]{1,3,2,0:T(8,128)(2,1)S(1)}, bf16[1,32,16,32]{1,3,2,0:T(8,128)(2,1)S(1)}, u32[]{:S(2)}, u32[]{:S(2)}) collective-permute-start(bf16[1,32,16,32]{1,3,2,0:T(8,128)(2,1)S(1)} %get-tuple-element.36), channel_id=1, source_target_pairs={{0,8},{8,16},{16,24},{1,9},{9,17},{17,25},{2,10},{10,18},{18,26},{... | collective-permute-start | bytes 98312 | tf_op jit(solution)/shard_map/ppermute | solution.py:18
  6.9 1.3 %collective-permute-start.1 = (bf16[1,32,16,32]{1,3,2,0:T(8,128)(2,1)S(1)}, bf16[1,32,16,32]{1,3,2,0:T(8,128)(2,1)S(1)}, u32[]{:S(2)}, u32[]{:S(2)}) collective-permute-start(bf16[1,32,16,32]{1,3,2,0:T(8,128)(2,1)S(1)} %get-tuple-element.37), channel_id=1, source_target_pairs={{8,0},{16,8},{24,16},{9,1},{17,9},{25,17},{10,2},{18,10},{26,18},{... | collective-permute-start | bytes 98312 | tf_op jit(solution)/shard_map/ppermute | solution.py:20
  8.2 1.4 %collective-permute-done = bf16[1,32,16,32]{1,3,2,0:T(8,128)(2,1)S(1)} collective-permute-done((bf16[1,32,16,32]{1,3,2,0:T(8,128)(2,1)S(1)}, bf16[1,32,16,32]{1,3,2,0:T(8,128)(2,1)S(1)}, u32[]{:S(2)}, u32[]{:S(2)}) %collective-permute-start) | collective-permute-done | bytes 32800 | tf_op jit(solution)/shard_map/ppermute | solution.py:18
  9.6 4.8 %collective-permute-done.1 = bf16[1,32,16,32]{1,3,2,0:T(8,128)(2,1)S(1)} collective-permute-done((bf16[1,32,16,32]{1,3,2,0:T(8,128)(2,1)S(1)}, bf16[1,32,16,32]{1,3,2,0:T(8,128)(2,1)S(1)}, u32[]{:S(2)}, u32[]{:S(2)}) %collective-permute-start.1) | collective-permute-done | bytes 32800 | tf_op jit(solution)/shard_map/ppermute | solution.py:20
  14.4 0.3 pad_maximum_fusion
  14.7 1.7 %fusion.43 = (bf16[10,1,16,32]{1,3,2,0:T(8,128)(2,1)}, bf16[10,1,16,32]{1,3,2,0:T(8,128)(2,1)S(1)}) fusion(bf16[10,32,16,32]{1,3,2,0:T(8,128)(2,1)S(1)} %pad_maximum_fusion), kind=kLoop, calls=%fused_computation.75 | loop fusion | bytes 40960 | tf_op jit(solution)/shard_map/slice | solution.py:15
  16.4 2.3 %copy.104 = bf16[10,1,16,32]{3,2,1,0:T(8,128)(2,1)S(1)} copy(bf16[10,1,16,32]{1,3,2,0:T(8,128)(2,1)} %get-tuple-element.32) | data formatting | bytes 20480 | tf_op jit(solution)/shard_map/slice | solution.py:15
  18.7 1.3 %collective-permute-start.2 = (bf16[10,1,16,32]{3,2,1,0:T(8,128)(2,1)S(1)}, bf16[10,1,16,32]{3,2,1,0:T(8,128)(2,1)S(1)}, u32[]{:S(2)}, u32[]{:S(2)}) collective-permute-start(bf16[10,1,16,32]{3,2,1,0:T(8,128)(2,1)S(1)} %copy.104), channel_id=1, source_target_pairs={{0,4},{1,5},{2,6},{3,7},{8,12},{9,13},{10,14},{11,15},{16,20},{17,... | collective-permute-start | bytes 30728 | tf_op jit(solution)/shard_map/ppermute | solution.py:18
  20.0 1.0 copy.105
  21.0 1.3 %collective-permute-start.3 = (bf16[10,1,16,32]{3,2,1,0:T(8,128)(2,1)S(1)}, bf16[10,1,16,32]{3,2,1,0:T(8,128)(2,1)S(1)}, u32[]{:S(2)}, u32[]{:S(2)}) collective-permute-start(bf16[10,1,16,32]{3,2,1,0:T(8,128)(2,1)S(1)} %copy.105), channel_id=1, source_target_pairs={{4,0},{5,1},{6,2},{7,3},{12,8},{13,9},{14,10},{15,11},{20,16},{21,... | collective-permute-start | bytes 30728 | tf_op jit(solution)/shard_map/ppermute | solution.py:20
  22.3 1.1 copy.106
  23.4 0.7 collective-permute-done.3
  24.1 2.1 %copy.107 = bf16[10,1,16,32]{1,3,2,0:T(8,128)(2,1)} copy(bf16[10,1,16,32]{3,2,1,0:T(8,128)(2,1)S(1)} %collective-permute-done.3) | data formatting | bytes 20480 | tf_op jit(solution)/shard_map/ppermute | solution.py:20
  26.2 1.2 pad_maximum_fusion.13
  27.4 3.5 %collective-permute-start.4 = (bf16[10,34,1,32]{1,3,2,0:T(8,128)(2,1)S(1)}, bf16[10,34,1,32]{1,3,2,0:T(8,128)(2,1)S(1)}, u32[]{:S(2)}, u32[]{:S(2)}) collective-permute-start(bf16[10,34,1,32]{1,3,2,0:T(8,128)(2,1)S(1)} %get-tuple-element.17), channel_id=1, source_target_pairs={{0,1},{1,2},{2,3},{4,5},{5,6},{6,7},{8,9},{9,10},{10,11},{12,13},{... | collective-permute-start | bytes 65288 | tf_op jit(solution)/shard_map/ppermute | solution.py:18
  30.9 1.5 %collective-permute-start.5 = (bf16[10,34,1,32]{1,3,2,0:T(8,128)(2,1)S(1)}, bf16[10,34,1,32]{1,3,2,0:T(8,128)(2,1)S(1)}, u32[]{:S(2)}, u32[]{:S(2)}) collective-permute-start(bf16[10,34,1,32]{1,3,2,0:T(8,128)(2,1)S(1)} %get-tuple-element.18), channel_id=1, source_target_pairs={{1,0},{2,1},{3,2},{5,4},{6,5},{7,6},{9,8},{10,9},{11,10},{13,12},{... | collective-permute-start | bytes 65288 | tf_op jit(solution)/shard_map/ppermute | solution.py:20
  32.4 0.7 collective-permute-done.4
  33.1 4.1 %collective-permute-done.5 = bf16[10,34,1,32]{1,3,2,0:T(8,128)(2,1)S(1)} collective-permute-done((bf16[10,34,1,32]{1,3,2,0:T(8,128)(2,1)S(1)}, bf16[10,34,1,32]{1,3,2,0:T(8,128)(2,1)S(1)}, u32[]{:S(2)}, u32[]{:S(2)}) %collective-permute-start.5) | collective-permute-done | bytes 21792 | tf_op jit(solution)/shard_map/ppermute | solution.py:20
  37.2 1.2 maximum_bitcast_fusion.1
  38.5 0.4 pad
  38.9 3.1 %copy.109 = bf16[10,34,1,8,3,32]{5,3,4,1,0,2:T(8,128)(2,1)} copy(bf16[10,34,1,8,3,32]{1,5,4,3,2,0:T(8,128)(2,1)S(1)} %bitcast.88) | data formatting | bytes 1044480 | tf_op jit(solution)/shard_map/conv_general_dilated | solution.py:28
  42.0 1.9 %slice.79 = bf16[10,34,1,7,2,32]{5,3,4,1,0,2:T(8,128)(2,1)S(1)} slice(bf16[10,34,1,8,3,32]{5,3,4,1,0,2:T(8,128)(2,1)} %copy.109), slice={[0:10], [0:34], [0:1], [1:8], [0:2], [0:32]} | slice | bytes 609280 | tf_op jit(solution)/shard_map/conv_general_dilated | solution.py:28
  43.8 0.1 copy-done.3
  44.0 4.4 %maximum_convert_fusion = bf16[8,32,8,3,32]{4,2,3,1,0:T(8,128)(2,1)S(1)} fusion(pred[8,3]{0,1:T(4,128)(4,1)S(1)} %copy-done.10, bf16[3,3,3,32,32]{4,3,2,1,0:T(8,128)(2,1)S(1)} %copy-done.6, bf16[10,34,1,7,2,32]{5,3,4,1,0,2:T(8,128)(2,1)S(1)} %slice.79, bf16[10,34,1,8,3,32]{5,3,4,1,0,2:T(8,128)(2,1)S(1)} %copy-done.3), kind=kOutput, calls=%fused_computation.16 | convolution fusion | flops 342939648 | bytes 1275416 | tf_op jit(solution)/shard_map/conv_general_dilated | solution.py:28
  48.4 0.3 copy.110
  48.7 1.6 %slice_convert_fusion = f32[8,32,1,16,32]{4,1,3,0,2:T(8,128)} fusion(bf16[8,32,1,24,32]{4,1,3,0,2:T(8,128)(2,1)S(1)} %bitcast.83), kind=kLoop, calls=%fused_computation.34 | loop fusion | flops 131072 | bytes 786432 | tf_op jit(solution)/shard_map/convert_element_type | solution.py:138
  50.3 2.2 %reduce_sum.37 = f32[2,4,2,2,2,32]{5,2,1,4,3,0:T(2,128)S(1)} reduce(f32[2,4,4,2,4,2,2,4,32]{8,4,3,2,7,6,5,1,0:T(4,128)} %bitcast.85, f32[]{:T(128)} %constant.12.clone.1), dimensions={1,4,7}, to_apply=%region_0.1 | reduce | flops 129024 | bytes 532484 | tf_op jit(solution)/shard_map/reduce_sum | solution.py:46
  52.6 0.1 fusion.42
  52.7 0.2 multiply_reduce_fusion
  53.4 0.2 convolution_convert_fusion.1
  53.6 0.2 convolution_convert_fusion
  53.8 0.1 reshape.109
  54.0 9.3 %all_to_all.33 = bf16[4,2,768]{2,1,0:T(2,128)(2,1)S(1)} all-to-all(bf16[4,2,768]{2,1,0:T(2,128)(2,1)S(1)} %reshape.145), channel_id=1, replica_groups=mesh['gx'=4,'gy'=2,'gz'=4] {'gz'}, dimensions={0} | all-to-all | bytes 24576 | tf_op jit(solution)/shard_map/all_to_all | solution.py:124
  63.5 9.6 %all_gather.3 = bf16[2,2,256,32]{3,1,0,2:T(2,128)(2,1)S(1)} all-gather(bf16[2,2,32,32]{3,1,0,2:T(2,128)(2,1)S(1)} %copy.118), channel_id=1, replica_groups=mesh['gx'=4,'gy'=2,'gz'=4] {'gx','gy'}, dimensions={2}, use_global_device_ids=true | all-gather | bytes 73728 | tf_op jit(solution)/shard_map/all_gather | solution.py:129
  73.0 0.2 fusion.46
  73.4 0.2 fusion.47
  73.6 0.2 fusion.27
  73.8 0.2 fusion.24
  74.1 7.9 %all_to_all.34 = bf16[4,2,256]{2,1,0:T(2,128)(2,1)S(1)} all-to-all(bf16[4,2,256]{2,1,0:T(2,128)(2,1)S(1)} %reshape.147), channel_id=1, replica_groups=mesh['gx'=4,'gy'=2,'gz'=4] {'gz'}, dimensions={0} | all-to-all | bytes 8192 | tf_op jit(solution)/shard_map/all_to_all | solution.py:131
  82.2 0.3 fusion.26
  82.6 0.5 broadcast_in_dim.35
  83.1 0.3 fusion.16
  83.5 2.2 %collective-permute-start.6 = (bf16[1,32,16,32]{3,1,2,0:T(8,128)(2,1)S(1)}, bf16[1,32,16,32]{3,1,2,0:T(8,128)(2,1)S(1)}, u32[]{:S(2)}, u32[]{:S(2)}) collective-permute-start(bf16[1,32,16,32]{3,1,2,0:T(8,128)(2,1)S(1)} %get-tuple-element.34), channel_id=1, source_target_pairs={{0,8},{8,16},{16,24},{1,9},{9,17},{17,25},{2,10},{10,18},{18,26},{... | collective-permute-start | bytes 98312 | tf_op jit(solution)/shard_map/ppermute | solution.py:18
  85.7 1.3 %collective-permute-start.7 = (bf16[1,32,16,32]{3,1,2,0:T(8,128)(2,1)S(1)}, bf16[1,32,16,32]{3,1,2,0:T(8,128)(2,1)S(1)}, u32[]{:S(2)}, u32[]{:S(2)}) collective-permute-start(bf16[1,32,16,32]{3,1,2,0:T(8,128)(2,1)S(1)} %get-tuple-element.35), channel_id=1, source_target_pairs={{8,0},{16,8},{24,16},{9,1},{17,9},{25,17},{10,2},{18,10},{26,18},{... | collective-permute-start | bytes 98312 | tf_op jit(solution)/shard_map/ppermute | solution.py:20
  87.0 1.2 collective-permute-done.6
  88.2 4.7 %collective-permute-done.7 = bf16[1,32,16,32]{3,1,2,0:T(8,128)(2,1)S(1)} collective-permute-done((bf16[1,32,16,32]{3,1,2,0:T(8,128)(2,1)S(1)}, bf16[1,32,16,32]{3,1,2,0:T(8,128)(2,1)S(1)}, u32[]{:S(2)}, u32[]{:S(2)}) %collective-permute-start.7) | collective-permute-done | bytes 32800 | tf_op jit(solution)/shard_map/ppermute | solution.py:20
  92.9 0.2 pad_maximum_fusion.8
  93.1 1.3 %collective-permute-start.8 = (bf16[10,1,16,32]{3,1,2,0:T(2,128)(2,1)S(1)}, bf16[10,1,16,32]{3,1,2,0:T(2,128)(2,1)S(1)}, u32[]{:S(2)}, u32[]{:S(2)}) collective-permute-start(bf16[10,1,16,32]{3,1,2,0:T(2,128)(2,1)S(1)} %get-tuple-element.28), channel_id=1, source_target_pairs={{0,4},{1,5},{2,6},{3,7},{8,12},{9,13},{10,14},{11,15},{16,20},{17,... | collective-permute-start | bytes 30728 | tf_op jit(solution)/shard_map/ppermute | solution.py:18
  94.4 1.3 %collective-permute-start.9 = (bf16[10,1,16,32]{3,1,2,0:T(2,128)(2,1)S(1)}, bf16[10,1,16,32]{3,1,2,0:T(2,128)(2,1)S(1)}, u32[]{:S(2)}, u32[]{:S(2)}) collective-permute-start(bf16[10,1,16,32]{3,1,2,0:T(2,128)(2,1)S(1)} %get-tuple-element.30), channel_id=1, source_target_pairs={{4,0},{5,1},{6,2},{7,3},{12,8},{13,9},{14,10},{15,11},{20,16},{21,... | collective-permute-start | bytes 30728 | tf_op jit(solution)/shard_map/ppermute | solution.py:20
  95.7 1.9 %collective-permute-done.9 = bf16[10,1,16,32]{3,1,2,0:T(2,128)(2,1)S(1)} collective-permute-done((bf16[10,1,16,32]{3,1,2,0:T(2,128)(2,1)S(1)}, bf16[10,1,16,32]{3,1,2,0:T(2,128)(2,1)S(1)}, u32[]{:S(2)}, u32[]{:S(2)}) %collective-permute-start.9) | collective-permute-done | bytes 10272 | tf_op jit(solution)/shard_map/ppermute | solution.py:20
  97.6 2.5 %collective-permute-start.10 = (bf16[10,34,1,32]{3,1,2,0:T(8,128)(2,1)S(1)}, bf16[10,34,1,32]{3,1,2,0:T(8,128)(2,1)S(1)}, u32[]{:S(2)}, u32[]{:S(2)}) collective-permute-start(bf16[10,34,1,32]{3,1,2,0:T(8,128)(2,1)S(1)} %get-tuple-element.19), channel_id=1, source_target_pairs={{0,1},{1,2},{2,3},{4,5},{5,6},{6,7},{8,9},{9,10},{10,11},{12,13},{... | collective-permute-start | bytes 65288 | tf_op jit(solution)/shard_map/ppermute | solution.py:18
  100.1 1.5 %collective-permute-start.11 = (bf16[10,34,1,32]{3,1,2,0:T(8,128)(2,1)S(1)}, bf16[10,34,1,32]{3,1,2,0:T(8,128)(2,1)S(1)}, u32[]{:S(2)}, u32[]{:S(2)}) collective-permute-start(bf16[10,34,1,32]{3,1,2,0:T(8,128)(2,1)S(1)} %get-tuple-element.20), channel_id=1, source_target_pairs={{1,0},{2,1},{3,2},{5,4},{6,5},{7,6},{9,8},{10,9},{11,10},{13,12},{... | collective-permute-start | bytes 65288 | tf_op jit(solution)/shard_map/ppermute | solution.py:20
  101.7 0.9 collective-permute-done.10
  102.6 4.1 %collective-permute-done.11 = bf16[10,34,1,32]{3,1,2,0:T(8,128)(2,1)S(1)} collective-permute-done((bf16[10,34,1,32]{3,1,2,0:T(8,128)(2,1)S(1)}, bf16[10,34,1,32]{3,1,2,0:T(8,128)(2,1)S(1)}, u32[]{:S(2)}, u32[]{:S(2)}) %collective-permute-start.11) | collective-permute-done | bytes 21792 | tf_op jit(solution)/shard_map/ppermute | solution.py:20
  106.7 2.1 %maximum_bitcast_fusion = bf16[10,34,1,18,32]{4,1,3,0,2:T(8,128)(2,1)S(1)} fusion(bf16[10,34,1,32]{3,1,2,0:T(8,128)(2,1)S(1)} %collective-permute-done.11, bf16[10,1,16,32]{3,1,2,0:T(2,128)(2,1)S(1)} %collective-permute-done.9, bf16[1,32,16,32]{3,1,2,0:T(8,128)(2,1)S(1)} %collective-permute-done.7, bf16[8,32,16,32]{3,1,2,0:T(8,128)(2,1)S(1)} %fusion.16, ...), kind=kLoop, calls=%fused_computation.19 | loop fusion | flops 2741760 | bytes 783360 | tf_op jit(solution)/shard_map/broadcast_in_dim | solution.py:29
  108.8 2.6 %copy.133 = bf16[10,34,1,18,32]{1,4,3,2,0:T(8,128)(2,1)} copy(bf16[10,34,1,18,32]{4,1,3,0,2:T(8,128)(2,1)S(1)} %maximum_bitcast_fusion) | data formatting | bytes 783360
  111.3 1.8 %pad.2.clone = bf16[10,34,1,24,32]{1,4,3,2,0:T(8,128)(2,1)S(1)} pad(bf16[10,34,1,18,32]{1,4,3,2,0:T(8,128)(2,1)} %copy.133, bf16[]{:T(256)} %constant.34), padding=0_0x0_0x0_0x0_6x0_0 | pad | bytes 913922 | tf_op jit(solution)/shard_map/broadcast_in_dim | solution.py:29
  113.1 3.1 %copy.128 = bf16[10,34,1,8,3,32]{5,3,4,1,0,2:T(8,128)(2,1)} copy(bf16[10,34,1,8,3,32]{1,5,4,3,2,0:T(8,128)(2,1)S(1)} %bitcast.87) | data formatting | bytes 1044480 | tf_op jit(solution)/shard_map/conv_general_dilated | solution.py:28
  116.3 1.9 %slice.87 = bf16[10,34,1,7,2,32]{5,3,4,1,0,2:T(8,128)(2,1)S(1)} slice(bf16[10,34,1,8,3,32]{5,3,4,1,0,2:T(8,128)(2,1)} %copy.128), slice={[0:10], [0:34], [0:1], [1:8], [0:2], [0:32]} | slice | bytes 609280 | tf_op jit(solution)/shard_map/conv_general_dilated | solution.py:28
  118.1 0.1 copy-done.2
  118.3 4.3 %select_convert_fusion = bf16[8,32,8,3,32]{4,2,3,1,0:T(8,128)(2,1)S(1)} fusion(pred[8,3]{0,1:T(4,128)(4,1)S(1)} %copy-done.10, bf16[3,3,3,32,32]{4,3,2,1,0:T(8,128)(2,1)S(1)} %copy-done.7, bf16[10,34,1,7,2,32]{5,3,4,1,0,2:T(8,128)(2,1)S(1)} %slice.87, bf16[10,34,1,8,3,32]{5,3,4,1,0,2:T(8,128)(2,1)S(1)} %copy-done.2), kind=kOutput, calls=%fused_computation.15 | convolution fusion | flops 342743040 | bytes 1275416 | tf_op jit(solution)/shard_map/conv_general_dilated | solution.py:28
  122.6 0.3 copy.129
  123.0 1.4 %copy.130 = bf16[8,32,16,32]{3,2,1,0:T(8,128)(2,1)} copy(bf16[8,32,16,32]{3,1,2,0:T(8,128)(2,1)S(1)} %slice_bitcast_fusion) | data formatting | bytes 524288 | tf_op jit(solution)/shard_map/convert_element_type | solution.py:140
  (55 shorter events, 1.6 us)
Async XLA Ops:
  0.0 53.6 %copy-start = (bf16[256,512]{1,0:T(8,128)(2,1)S(1)}, bf16[256,512]{1,0:T(8,128)(2,1)}, u32[]{:S(2)}) copy-start(bf16[256,512]{1,0:T(8,128)(2,1)} %param.13) | copy-start | bytes 786436
  2.0 7.6 %collective-permute-start = (bf16[1,32,16,32]{1,3,2,0:T(8,128)(2,1)S(1)}, bf16[1,32,16,32]{1,3,2,0:T(8,128)(2,1)S(1)}, u32[]{:S(2)}, u32[]{:S(2)}) collective-permute-start(bf16[1,32,16,32]{1,3,2,0:T(8,128)(2,1)S(1)} %get-tuple-element.36), channel_id=1, source_target_pairs={{0,8},{8,16},{16,24},{1,9},{9,17},{17,25},{2,10},{10,18},{18,26},{... | collective-permute-start | bytes 98312 | tf_op jit(solution)/shard_map/ppermute | solution.py:18
  6.9 7.5 %collective-permute-start.1 = (bf16[1,32,16,32]{1,3,2,0:T(8,128)(2,1)S(1)}, bf16[1,32,16,32]{1,3,2,0:T(8,128)(2,1)S(1)}, u32[]{:S(2)}, u32[]{:S(2)}) collective-permute-start(bf16[1,32,16,32]{1,3,2,0:T(8,128)(2,1)S(1)} %get-tuple-element.37), channel_id=1, source_target_pairs={{8,0},{16,8},{24,16},{9,1},{17,9},{25,17},{10,2},{18,10},{26,18},{... | collective-permute-start | bytes 98312 | tf_op jit(solution)/shard_map/ppermute | solution.py:20
  18.7 3.6 %collective-permute-start.2 = (bf16[10,1,16,32]{3,2,1,0:T(8,128)(2,1)S(1)}, bf16[10,1,16,32]{3,2,1,0:T(8,128)(2,1)S(1)}, u32[]{:S(2)}, u32[]{:S(2)}) collective-permute-start(bf16[10,1,16,32]{3,2,1,0:T(8,128)(2,1)S(1)} %copy.104), channel_id=1, source_target_pairs={{0,4},{1,5},{2,6},{3,7},{8,12},{9,13},{10,14},{11,15},{16,20},{17,... | collective-permute-start | bytes 30728 | tf_op jit(solution)/shard_map/ppermute | solution.py:18
  21.0 3.1 %collective-permute-start.3 = (bf16[10,1,16,32]{3,2,1,0:T(8,128)(2,1)S(1)}, bf16[10,1,16,32]{3,2,1,0:T(8,128)(2,1)S(1)}, u32[]{:S(2)}, u32[]{:S(2)}) collective-permute-start(bf16[10,1,16,32]{3,2,1,0:T(8,128)(2,1)S(1)} %copy.105), channel_id=1, source_target_pairs={{4,0},{5,1},{6,2},{7,3},{12,8},{13,9},{14,10},{15,11},{20,16},{21,... | collective-permute-start | bytes 30728 | tf_op jit(solution)/shard_map/ppermute | solution.py:20
  26.2 11.0 %copy-start.1 = (bf16[10,1,16,32]{1,3,2,0:T(8,128)(2,1)S(1)}, bf16[10,1,16,32]{1,3,2,0:T(8,128)(2,1)}, u32[]{:S(2)}) copy-start(bf16[10,1,16,32]{1,3,2,0:T(8,128)(2,1)} %copy.107) | copy-start | bytes 30724
  27.4 5.7 %collective-permute-start.4 = (bf16[10,34,1,32]{1,3,2,0:T(8,128)(2,1)S(1)}, bf16[10,34,1,32]{1,3,2,0:T(8,128)(2,1)S(1)}, u32[]{:S(2)}, u32[]{:S(2)}) collective-permute-start(bf16[10,34,1,32]{1,3,2,0:T(8,128)(2,1)S(1)} %get-tuple-element.17), channel_id=1, source_target_pairs={{0,1},{1,2},{2,3},{4,5},{5,6},{6,7},{8,9},{9,10},{10,11},{12,13},{... | collective-permute-start | bytes 65288 | tf_op jit(solution)/shard_map/ppermute | solution.py:18
  30.9 6.3 %collective-permute-start.5 = (bf16[10,34,1,32]{1,3,2,0:T(8,128)(2,1)S(1)}, bf16[10,34,1,32]{1,3,2,0:T(8,128)(2,1)S(1)}, u32[]{:S(2)}, u32[]{:S(2)}) collective-permute-start(bf16[10,34,1,32]{1,3,2,0:T(8,128)(2,1)S(1)} %get-tuple-element.18), channel_id=1, source_target_pairs={{1,0},{2,1},{3,2},{5,4},{6,5},{7,6},{9,8},{10,9},{11,10},{13,12},{... | collective-permute-start | bytes 65288 | tf_op jit(solution)/shard_map/ppermute | solution.py:20
  42.0 2.0 %copy-start.3 = (bf16[10,34,1,8,3,32]{5,3,4,1,0,2:T(8,128)(2,1)S(1)}, bf16[10,34,1,8,3,32]{5,3,4,1,0,2:T(8,128)(2,1)}, u32[]{:S(2)}) copy-start(bf16[10,34,1,8,3,32]{5,3,4,1,0,2:T(8,128)(2,1)} %copy.109) | copy-start | bytes 1566724
  42.0 2.0 %copy-start.6 = (bf16[3,3,3,32,32]{4,3,2,1,0:T(8,128)(2,1)S(1)}, bf16[3,3,3,32,32]{4,3,2,1,0:T(8,128)(2,1)}, u32[]{:S(2)}) copy-start(bf16[3,3,3,32,32]{4,3,2,1,0:T(8,128)(2,1)} %param.9) | copy-start | bytes 165892
  42.0 2.0 %copy-start.10 = (pred[8,3]{0,1:T(4,128)(4,1)S(1)}, pred[8,3]{0,1:T(4,128)(4,1)}, u32[]{:S(2)}) copy-start(pred[8,3]{0,1:T(4,128)(4,1)} %constant.42) | copy-start | bytes 76
  48.7 4.7 %copy-start.8 = (bf16[256,256]{1,0:T(8,128)(2,1)S(1)}, bf16[256,256]{1,0:T(8,128)(2,1)}, u32[]{:S(2)}) copy-start(bf16[256,256]{1,0:T(8,128)(2,1)} %param.12) | copy-start | bytes 393220
  48.7 4.7 %copy-start.9 = (f32[256]{0:T(256)S(1)}, f32[256]{0:T(256)}, u32[]{:S(2)}) copy-start(f32[256]{0:T(256)} %param.11) | copy-start | bytes 3076
  50.3 31.9 %copy-start.4 = (bf16[256,256]{1,0:T(8,128)(2,1)S(1)}, bf16[256,256]{1,0:T(8,128)(2,1)}, u32[]{:S(2)}) copy-start(bf16[256,256]{1,0:T(8,128)(2,1)} %param.15) | copy-start | bytes 393220
  50.3 31.9 %copy-start.5 = (bf16[256,256]{1,0:T(8,128)(2,1)S(1)}, bf16[256,256]{1,0:T(8,128)(2,1)}, u32[]{:S(2)}) copy-start(bf16[256,256]{1,0:T(8,128)(2,1)} %param.14) | copy-start | bytes 393220
  83.5 4.7 %collective-permute-start.6 = (bf16[1,32,16,32]{3,1,2,0:T(8,128)(2,1)S(1)}, bf16[1,32,16,32]{3,1,2,0:T(8,128)(2,1)S(1)}, u32[]{:S(2)}, u32[]{:S(2)}) collective-permute-start(bf16[1,32,16,32]{3,1,2,0:T(8,128)(2,1)S(1)} %get-tuple-element.34), channel_id=1, source_target_pairs={{0,8},{8,16},{16,24},{1,9},{9,17},{17,25},{2,10},{10,18},{18,26},{... | collective-permute-start | bytes 98312 | tf_op jit(solution)/shard_map/ppermute | solution.py:18
  85.7 7.2 %collective-permute-start.7 = (bf16[1,32,16,32]{3,1,2,0:T(8,128)(2,1)S(1)}, bf16[1,32,16,32]{3,1,2,0:T(8,128)(2,1)S(1)}, u32[]{:S(2)}, u32[]{:S(2)}) collective-permute-start(bf16[1,32,16,32]{3,1,2,0:T(8,128)(2,1)S(1)} %get-tuple-element.35), channel_id=1, source_target_pairs={{8,0},{16,8},{24,16},{9,1},{17,9},{25,17},{10,2},{18,10},{26,18},{... | collective-permute-start | bytes 98312 | tf_op jit(solution)/shard_map/ppermute | solution.py:20
  93.1 2.6 %collective-permute-start.8 = (bf16[10,1,16,32]{3,1,2,0:T(2,128)(2,1)S(1)}, bf16[10,1,16,32]{3,1,2,0:T(2,128)(2,1)S(1)}, u32[]{:S(2)}, u32[]{:S(2)}) collective-permute-start(bf16[10,1,16,32]{3,1,2,0:T(2,128)(2,1)S(1)} %get-tuple-element.28), channel_id=1, source_target_pairs={{0,4},{1,5},{2,6},{3,7},{8,12},{9,13},{10,14},{11,15},{16,20},{17,... | collective-permute-start | bytes 30728 | tf_op jit(solution)/shard_map/ppermute | solution.py:18
  94.4 3.2 %collective-permute-start.9 = (bf16[10,1,16,32]{3,1,2,0:T(2,128)(2,1)S(1)}, bf16[10,1,16,32]{3,1,2,0:T(2,128)(2,1)S(1)}, u32[]{:S(2)}, u32[]{:S(2)}) collective-permute-start(bf16[10,1,16,32]{3,1,2,0:T(2,128)(2,1)S(1)} %get-tuple-element.30), channel_id=1, source_target_pairs={{4,0},{5,1},{6,2},{7,3},{12,8},{13,9},{14,10},{15,11},{20,16},{21,... | collective-permute-start | bytes 30728 | tf_op jit(solution)/shard_map/ppermute | solution.py:20
  97.6 4.9 %collective-permute-start.10 = (bf16[10,34,1,32]{3,1,2,0:T(8,128)(2,1)S(1)}, bf16[10,34,1,32]{3,1,2,0:T(8,128)(2,1)S(1)}, u32[]{:S(2)}, u32[]{:S(2)}) collective-permute-start(bf16[10,34,1,32]{3,1,2,0:T(8,128)(2,1)S(1)} %get-tuple-element.19), channel_id=1, source_target_pairs={{0,1},{1,2},{2,3},{4,5},{5,6},{6,7},{8,9},{9,10},{10,11},{12,13},{... | collective-permute-start | bytes 65288 | tf_op jit(solution)/shard_map/ppermute | solution.py:18
  100.1 6.6 %collective-permute-start.11 = (bf16[10,34,1,32]{3,1,2,0:T(8,128)(2,1)S(1)}, bf16[10,34,1,32]{3,1,2,0:T(8,128)(2,1)S(1)}, u32[]{:S(2)}, u32[]{:S(2)}) collective-permute-start(bf16[10,34,1,32]{3,1,2,0:T(8,128)(2,1)S(1)} %get-tuple-element.20), channel_id=1, source_target_pairs={{1,0},{2,1},{3,2},{5,4},{6,5},{7,6},{9,8},{10,9},{11,10},{13,12},{... | collective-permute-start | bytes 65288 | tf_op jit(solution)/shard_map/ppermute | solution.py:20
  116.3 2.0 %copy-start.2 = (bf16[10,34,1,8,3,32]{5,3,4,1,0,2:T(8,128)(2,1)S(1)}, bf16[10,34,1,8,3,32]{5,3,4,1,0,2:T(8,128)(2,1)}, u32[]{:S(2)}) copy-start(bf16[10,34,1,8,3,32]{5,3,4,1,0,2:T(8,128)(2,1)} %copy.128) | copy-start | bytes 1566724
  116.3 2.0 %copy-start.7 = (bf16[3,3,3,32,32]{4,3,2,1,0:T(8,128)(2,1)S(1)}, bf16[3,3,3,32,32]{4,3,2,1,0:T(8,128)(2,1)}, u32[]{:S(2)}) copy-start(bf16[3,3,3,32,32]{4,3,2,1,0:T(8,128)(2,1)} %param.10) | copy-start | bytes 165892
where the time goes:
time: 125 us; the launch traced here: 124 us
  local copies, waits for them, and re-layouts  29.4 us (24%)
  blocking collectives  26.7 us (21%)
  waiting for transfers between devices  24.6 us (20%)
  starting transfers between devices  23.8 us (19%)
  matrix products  9.77 us (8%)
  other arithmetic  9.75 us (8%)
    ppermute x6, waiting for transfers between devices, with_halo(): lax.ppermute(head, axis, [((i + 1) % count, i) for i in range(ends)])  20.3 us
    ppermute x6, starting transfers between devices, with_halo(): lax.ppermute(tail, axis, [(i, (i + 1) % count) for i in range(ends)])  15.6 us
    conv_general_dilated x4, local copies, waits for them, and re-layouts, convolve(): lax.conv_general_dilated(padded[None], kernel, (1, 1, 1), 'VALID', dimens...  9.95 us
    all_gather x1, blocking collectives, on_device(): lax.all_gather(arranged[1:], ('gx', 'gy'), axis=2, tiled=True)  9.56 us
    all_to_all x1, blocking collectives, on_device(): lax.all_to_all(packed, 'gz', split_axis=1, concat_axis=2, tiled=True)  9.26 us
    conv_general_dilated x2, matrix products, convolve(): lax.conv_general_dilated(padded[None], kernel, (1, 1, 1), 'VALID', dimens...  8.72 us
    ppermute x6, starting transfers between devices, with_halo(): lax.ppermute(head, axis, [((i + 1) % count, i) for i in range(ends)])  8.15 us
    all_to_all x1, blocking collectives, on_device(): lax.all_to_all(finish(running), 'gz', split_axis=1, concat_axis=0, tiled=...  7.91 us
  transfers between devices with their start and end apart: 12, of which 10 were waited for; matrix products, arithmetic and copies ran while one was open for 2% of the time, Pallas kernels for 0%

commit v1 on v0

--- a/solution.py
+++ b/solution.py
@@ -128,7 +128,11 @@
         start_state(head_queries),
         lax.all_gather(arranged[1:], ("gx", "gy"), axis=2, tiled=True),
     )
-    returned = lax.all_to_all(finish(running), "gz", split_axis=1, concat_axis=0, tiled=True)
+    block = finish(running)
+    peers = lax.axis_size("gz")
+    blocks = jnp.stack(jnp.split(block, peers, axis=1), axis=0)
+    blocks = lax.all_to_all(blocks, "gz", split_axis=0, concat_axis=0)
+    returned = jnp.concatenate(blocks, axis=0)
     attended = returned.transpose(1, 0, 2).reshape(token_count, width)
     mixture = (tokens + jnp.dot(attended, out_weight, preferred_element_type=jnp.float32)).astype(
         jnp.bfloat16

time: 125 us -> 125 us (level)
  no operation moved by 1% of the time
where the time goes in v1:
time: 125 us; the launch traced here: 124 us
  local copies, waits for them, and re-layouts  29.3 us (23%)
  blocking collectives  26.7 us (21%)
  waiting for transfers between devices  24.6 us (20%)
  starting transfers between devices  23.8 us (19%)
  matrix products  9.77 us (8%)
  other arithmetic  9.75 us (8%)
    ppermute x6, waiting for transfers between devices, with_halo(): lax.ppermute(head, axis, [((i + 1) % count, i) for i in range(ends)])  20.3 us
    ppermute x6, starting transfers between devices, with_halo(): lax.ppermute(tail, axis, [(i, (i + 1) % count) for i in range(ends)])  15.6 us
    conv_general_dilated x4, local copies, waits for them, and re-layouts, convolve(): lax.conv_general_dilated(padded[None], kernel, (1, 1, 1), 'VALID', dimens...  9.9 us
    all_gather x1, blocking collectives, on_device(): lax.all_gather(arranged[1:], ('gx', 'gy'), axis=2, tiled=True)  9.56 us
    all_to_all x1, blocking collectives, on_device(): lax.all_to_all(packed, 'gz', split_axis=1, concat_axis=2, tiled=True)  9.26 us
    conv_general_dilated x2, matrix products, convolve(): lax.conv_general_dilated(padded[None], kernel, (1, 1, 1), 'VALID', dimens...  8.72 us
    ppermute x6, starting transfers between devices, with_halo(): lax.ppermute(head, axis, [((i + 1) % count, i) for i in range(ends)])  8.15 us
    all_to_all x1, blocking collectives, on_device(): blocks = lax.all_to_all(blocks, 'gz', split_axis=0, concat_axis=0)  7.91 us
  transfers between devices with their start and end apart: 12, of which 10 were waited for; matrix products, arithmetic and copies ran while one was open for 2% of the time, Pallas kernels for 0%

profile of v1, /device:TPU:0, one launch (start us, length us, event | category | flops | bytes accessed | tf_op | source)
XLA Modules:
  0.0 124.3 jit_solution(3559177864279818619)
XLA Ops:
  0.0 2.0 %copy.69 = bf16[8,32,16,32]{1,3,2,0:T(8,128)(2,1)S(1)} copy(bf16[8,32,16,32]{3,2,1,0:T(8,128)(2,1)} %param.8) | data formatting | bytes 524288 | tf_op args[0]
  2.0 4.9 %collective-permute-start = (bf16[1,32,16,32]{1,3,2,0:T(8,128)(2,1)S(1)}, bf16[1,32,16,32]{1,3,2,0:T(8,128)(2,1)S(1)}, u32[]{:S(2)}, u32[]{:S(2)}) collective-permute-start(bf16[1,32,16,32]{1,3,2,0:T(8,128)(2,1)S(1)} %get-tuple-element.36), channel_id=1, source_target_pairs={{0,8},{8,16},{16,24},{1,9},{9,17},{17,25},{2,10},{10,18},{18,26},{... | collective-permute-start | bytes 98312 | tf_op jit(solution)/shard_map/ppermute | solution.py:18
  6.9 1.3 %collective-permute-start.1 = (bf16[1,32,16,32]{1,3,2,0:T(8,128)(2,1)S(1)}, bf16[1,32,16,32]{1,3,2,0:T(8,128)(2,1)S(1)}, u32[]{:S(2)}, u32[]{:S(2)}) collective-permute-start(bf16[1,32,16,32]{1,3,2,0:T(8,128)(2,1)S(1)} %get-tuple-element.37), channel_id=1, source_target_pairs={{8,0},{16,8},{24,16},{9,1},{17,9},{25,17},{10,2},{18,10},{26,18},{... | collective-permute-start | bytes 98312 | tf_op jit(solution)/shard_map/ppermute | solution.py:20
  8.2 1.4 %collective-permute-done = bf16[1,32,16,32]{1,3,2,0:T(8,128)(2,1)S(1)} collective-permute-done((bf16[1,32,16,32]{1,3,2,0:T(8,128)(2,1)S(1)}, bf16[1,32,16,32]{1,3,2,0:T(8,128)(2,1)S(1)}, u32[]{:S(2)}, u32[]{:S(2)}) %collective-permute-start) | collective-permute-done | bytes 32800 | tf_op jit(solution)/shard_map/ppermute | solution.py:18
  9.6 4.8 %collective-permute-done.1 = bf16[1,32,16,32]{1,3,2,0:T(8,128)(2,1)S(1)} collective-permute-done((bf16[1,32,16,32]{1,3,2,0:T(8,128)(2,1)S(1)}, bf16[1,32,16,32]{1,3,2,0:T(8,128)(2,1)S(1)}, u32[]{:S(2)}, u32[]{:S(2)}) %collective-permute-start.1) | collective-permute-done | bytes 32800 | tf_op jit(solution)/shard_map/ppermute | solution.py:20
  14.4 0.3 pad_maximum_fusion
  14.7 1.7 %fusion.43 = (bf16[10,1,16,32]{1,3,2,0:T(8,128)(2,1)}, bf16[10,1,16,32]{1,3,2,0:T(8,128)(2,1)S(1)}) fusion(bf16[10,32,16,32]{1,3,2,0:T(8,128)(2,1)S(1)} %pad_maximum_fusion), kind=kLoop, calls=%fused_computation.80 | loop fusion | bytes 40960 | tf_op jit(solution)/shard_map/slice | solution.py:15
  16.4 2.3 %copy.72 = bf16[10,1,16,32]{3,2,1,0:T(8,128)(2,1)S(1)} copy(bf16[10,1,16,32]{1,3,2,0:T(8,128)(2,1)} %get-tuple-element.32) | data formatting | bytes 20480 | tf_op jit(solution)/shard_map/slice | solution.py:15
  18.7 1.3 %collective-permute-start.2 = (bf16[10,1,16,32]{3,2,1,0:T(8,128)(2,1)S(1)}, bf16[10,1,16,32]{3,2,1,0:T(8,128)(2,1)S(1)}, u32[]{:S(2)}, u32[]{:S(2)}) collective-permute-start(bf16[10,1,16,32]{3,2,1,0:T(8,128)(2,1)S(1)} %copy.72), channel_id=1, source_target_pairs={{0,4},{1,5},{2,6},{3,7},{8,12},{9,13},{10,14},{11,15},{16,20},{17,... | collective-permute-start | bytes 30728 | tf_op jit(solution)/shard_map/ppermute | solution.py:18
  20.0 1.0 copy.73
  21.0 1.3 %collective-permute-start.3 = (bf16[10,1,16,32]{3,2,1,0:T(8,128)(2,1)S(1)}, bf16[10,1,16,32]{3,2,1,0:T(8,128)(2,1)S(1)}, u32[]{:S(2)}, u32[]{:S(2)}) collective-permute-start(bf16[10,1,16,32]{3,2,1,0:T(8,128)(2,1)S(1)} %copy.73), channel_id=1, source_target_pairs={{4,0},{5,1},{6,2},{7,3},{12,8},{13,9},{14,10},{15,11},{20,16},{21,... | collective-permute-start | bytes 30728 | tf_op jit(solution)/shard_map/ppermute | solution.py:20
  22.3 1.1 copy.74
  23.4 0.7 collective-permute-done.3
  24.1 2.1 %copy.75 = bf16[10,1,16,32]{1,3,2,0:T(8,128)(2,1)} copy(bf16[10,1,16,32]{3,2,1,0:T(8,128)(2,1)S(1)} %collective-permute-done.3) | data formatting | bytes 20480 | tf_op jit(solution)/shard_map/ppermute | solution.py:20
  26.2 1.2 pad_maximum_fusion.13
  27.4 3.5 %collective-permute-start.4 = (bf16[10,34,1,32]{1,3,2,0:T(8,128)(2,1)S(1)}, bf16[10,34,1,32]{1,3,2,0:T(8,128)(2,1)S(1)}, u32[]{:S(2)}, u32[]{:S(2)}) collective-permute-start(bf16[10,34,1,32]{1,3,2,0:T(8,128)(2,1)S(1)} %get-tuple-element.17), channel_id=1, source_target_pairs={{0,1},{1,2},{2,3},{4,5},{5,6},{6,7},{8,9},{9,10},{10,11},{12,13},{... | collective-permute-start | bytes 65288 | tf_op jit(solution)/shard_map/ppermute | solution.py:18
  30.9 1.5 %collective-permute-start.5 = (bf16[10,34,1,32]{1,3,2,0:T(8,128)(2,1)S(1)}, bf16[10,34,1,32]{1,3,2,0:T(8,128)(2,1)S(1)}, u32[]{:S(2)}, u32[]{:S(2)}) collective-permute-start(bf16[10,34,1,32]{1,3,2,0:T(8,128)(2,1)S(1)} %get-tuple-element.18), channel_id=1, source_target_pairs={{1,0},{2,1},{3,2},{5,4},{6,5},{7,6},{9,8},{10,9},{11,10},{13,12},{... | collective-permute-start | bytes 65288 | tf_op jit(solution)/shard_map/ppermute | solution.py:20
  32.4 0.7 collective-permute-done.4
  33.2 4.1 %collective-permute-done.5 = bf16[10,34,1,32]{1,3,2,0:T(8,128)(2,1)S(1)} collective-permute-done((bf16[10,34,1,32]{1,3,2,0:T(8,128)(2,1)S(1)}, bf16[10,34,1,32]{1,3,2,0:T(8,128)(2,1)S(1)}, u32[]{:S(2)}, u32[]{:S(2)}) %collective-permute-start.5) | collective-permute-done | bytes 21792 | tf_op jit(solution)/shard_map/ppermute | solution.py:20
  37.3 1.2 maximum_bitcast_fusion.1
  38.5 0.4 pad
  38.9 3.1 %copy.77 = bf16[10,34,1,8,3,32]{5,3,4,1,0,2:T(8,128)(2,1)} copy(bf16[10,34,1,8,3,32]{1,5,4,3,2,0:T(8,128)(2,1)S(1)} %bitcast.88) | data formatting | bytes 1044480 | tf_op jit(solution)/shard_map/conv_general_dilated | solution.py:28
  42.0 1.9 %slice.79 = bf16[10,34,1,7,2,32]{5,3,4,1,0,2:T(8,128)(2,1)S(1)} slice(bf16[10,34,1,8,3,32]{5,3,4,1,0,2:T(8,128)(2,1)} %copy.77), slice={[0:10], [0:34], [0:1], [1:8], [0:2], [0:32]} | slice | bytes 609280 | tf_op jit(solution)/shard_map/conv_general_dilated | solution.py:28
  43.8 0.1 copy-done.3
  44.0 4.4 %maximum_convert_fusion = bf16[8,32,8,3,32]{4,2,3,1,0:T(8,128)(2,1)S(1)} fusion(pred[8,3]{0,1:T(4,128)(4,1)S(1)} %copy-done.10, bf16[3,3,3,32,32]{4,3,2,1,0:T(8,128)(2,1)S(1)} %copy-done.6, bf16[10,34,1,7,2,32]{5,3,4,1,0,2:T(8,128)(2,1)S(1)} %slice.79, bf16[10,34,1,8,3,32]{5,3,4,1,0,2:T(8,128)(2,1)S(1)} %copy-done.3), kind=kOutput, calls=%fused_computation.16 | convolution fusion | flops 342939648 | bytes 1275416 | tf_op jit(solution)/shard_map/conv_general_dilated | solution.py:28
  48.4 0.3 copy.78
  48.7 1.6 %slice_convert_fusion = f32[8,32,1,16,32]{4,1,3,0,2:T(8,128)} fusion(bf16[8,32,1,24,32]{4,1,3,0,2:T(8,128)(2,1)S(1)} %bitcast.83), kind=kLoop, calls=%fused_computation.34 | loop fusion | flops 131072 | bytes 786432 | tf_op jit(solution)/shard_map/convert_element_type | solution.py:142
  50.3 2.2 %reduce_sum.37 = f32[2,4,2,2,2,32]{5,2,1,4,3,0:T(2,128)S(1)} reduce(f32[2,4,4,2,4,2,2,4,32]{8,4,3,2,7,6,5,1,0:T(4,128)} %bitcast.85, f32[]{:T(128)} %constant.12.clone.1), dimensions={1,4,7}, to_apply=%region_0.1 | reduce | flops 129024 | bytes 532484 | tf_op jit(solution)/shard_map/reduce_sum | solution.py:46
  52.6 0.1 fusion.42
  52.7 0.2 multiply_reduce_fusion
  53.4 0.2 convolution_convert_fusion.1
  53.6 0.2 convolution_convert_fusion
  53.8 0.1 reshape.112
  54.0 9.3 %all_to_all.20 = bf16[4,2,768]{2,1,0:T(2,128)(2,1)S(1)} all-to-all(bf16[4,2,768]{2,1,0:T(2,128)(2,1)S(1)} %reshape.149), channel_id=1, replica_groups=mesh['gx'=4,'gy'=2,'gz'=4] {'gz'}, dimensions={0} | all-to-all | bytes 24576 | tf_op jit(solution)/shard_map/all_to_all | solution.py:124
  63.5 9.6 %all_gather.3 = bf16[2,2,256,32]{3,1,0,2:T(2,128)(2,1)S(1)} all-gather(bf16[2,2,32,32]{3,1,0,2:T(2,128)(2,1)S(1)} %copy.86), channel_id=1, replica_groups=mesh['gx'=4,'gy'=2,'gz'=4] {'gx','gy'}, dimensions={2}, use_global_device_ids=true | all-gather | bytes 73728 | tf_op jit(solution)/shard_map/all_gather | solution.py:129
  73.0 0.2 fusion.46
  73.4 0.2 fusion.47
  73.6 0.2 fusion.27
  73.8 0.2 fusion.24
  74.1 7.9 %all_to_all.21 = bf16[4,2,256]{2,1,0:T(2,128)(2,1)S(1)} all-to-all(bf16[4,2,256]{2,1,0:T(2,128)(2,1)S(1)} %reshape.151), channel_id=1, replica_groups=mesh['gx'=4,'gy'=2,'gz'=4] {'gz'}, dimensions={0} | all-to-all | bytes 8192 | tf_op jit(solution)/shard_map/all_to_all | solution.py:134
  82.2 0.3 fusion.26
  82.6 0.5 broadcast_in_dim.35
  83.1 0.3 fusion.16
  83.5 2.2 %collective-permute-start.6 = (bf16[1,32,16,32]{3,1,2,0:T(8,128)(2,1)S(1)}, bf16[1,32,16,32]{3,1,2,0:T(8,128)(2,1)S(1)}, u32[]{:S(2)}, u32[]{:S(2)}) collective-permute-start(bf16[1,32,16,32]{3,1,2,0:T(8,128)(2,1)S(1)} %get-tuple-element.34), channel_id=1, source_target_pairs={{0,8},{8,16},{16,24},{1,9},{9,17},{17,25},{2,10},{10,18},{18,26},{... | collective-permute-start | bytes 98312 | tf_op jit(solution)/shard_map/ppermute | solution.py:18
  85.7 1.3 %collective-permute-start.7 = (bf16[1,32,16,32]{3,1,2,0:T(8,128)(2,1)S(1)}, bf16[1,32,16,32]{3,1,2,0:T(8,128)(2,1)S(1)}, u32[]{:S(2)}, u32[]{:S(2)}) collective-permute-start(bf16[1,32,16,32]{3,1,2,0:T(8,128)(2,1)S(1)} %get-tuple-element.35), channel_id=1, source_target_pairs={{8,0},{16,8},{24,16},{9,1},{17,9},{25,17},{10,2},{18,10},{26,18},{... | collective-permute-start | bytes 98312 | tf_op jit(solution)/shard_map/ppermute | solution.py:20
  87.0 1.2 collective-permute-done.6
  88.2 4.7 %collective-permute-done.7 = bf16[1,32,16,32]{3,1,2,0:T(8,128)(2,1)S(1)} collective-permute-done((bf16[1,32,16,32]{3,1,2,0:T(8,128)(2,1)S(1)}, bf16[1,32,16,32]{3,1,2,0:T(8,128)(2,1)S(1)}, u32[]{:S(2)}, u32[]{:S(2)}) %collective-permute-start.7) | collective-permute-done | bytes 32800 | tf_op jit(solution)/shard_map/ppermute | solution.py:20
  92.9 0.2 pad_maximum_fusion.8
  93.0 1.3 %collective-permute-start.8 = (bf16[10,1,16,32]{3,1,2,0:T(2,128)(2,1)S(1)}, bf16[10,1,16,32]{3,1,2,0:T(2,128)(2,1)S(1)}, u32[]{:S(2)}, u32[]{:S(2)}) collective-permute-start(bf16[10,1,16,32]{3,1,2,0:T(2,128)(2,1)S(1)} %get-tuple-element.28), channel_id=1, source_target_pairs={{0,4},{1,5},{2,6},{3,7},{8,12},{9,13},{10,14},{11,15},{16,20},{17,... | collective-permute-start | bytes 30728 | tf_op jit(solution)/shard_map/ppermute | solution.py:18
  94.3 1.3 %collective-permute-start.9 = (bf16[10,1,16,32]{3,1,2,0:T(2,128)(2,1)S(1)}, bf16[10,1,16,32]{3,1,2,0:T(2,128)(2,1)S(1)}, u32[]{:S(2)}, u32[]{:S(2)}) collective-permute-start(bf16[10,1,16,32]{3,1,2,0:T(2,128)(2,1)S(1)} %get-tuple-element.30), channel_id=1, source_target_pairs={{4,0},{5,1},{6,2},{7,3},{12,8},{13,9},{14,10},{15,11},{20,16},{21,... | collective-permute-start | bytes 30728 | tf_op jit(solution)/shard_map/ppermute | solution.py:20
  95.6 1.9 %collective-permute-done.9 = bf16[10,1,16,32]{3,1,2,0:T(2,128)(2,1)S(1)} collective-permute-done((bf16[10,1,16,32]{3,1,2,0:T(2,128)(2,1)S(1)}, bf16[10,1,16,32]{3,1,2,0:T(2,128)(2,1)S(1)}, u32[]{:S(2)}, u32[]{:S(2)}) %collective-permute-start.9) | collective-permute-done | bytes 10272 | tf_op jit(solution)/shard_map/ppermute | solution.py:20
  97.6 2.5 %collective-permute-start.10 = (bf16[10,34,1,32]{3,1,2,0:T(8,128)(2,1)S(1)}, bf16[10,34,1,32]{3,1,2,0:T(8,128)(2,1)S(1)}, u32[]{:S(2)}, u32[]{:S(2)}) collective-permute-start(bf16[10,34,1,32]{3,1,2,0:T(8,128)(2,1)S(1)} %get-tuple-element.19), channel_id=1, source_target_pairs={{0,1},{1,2},{2,3},{4,5},{5,6},{6,7},{8,9},{9,10},{10,11},{12,13},{... | collective-permute-start | bytes 65288 | tf_op jit(solution)/shard_map/ppermute | solution.py:18
  100.1 1.5 %collective-permute-start.11 = (bf16[10,34,1,32]{3,1,2,0:T(8,128)(2,1)S(1)}, bf16[10,34,1,32]{3,1,2,0:T(8,128)(2,1)S(1)}, u32[]{:S(2)}, u32[]{:S(2)}) collective-permute-start(bf16[10,34,1,32]{3,1,2,0:T(8,128)(2,1)S(1)} %get-tuple-element.20), channel_id=1, source_target_pairs={{1,0},{2,1},{3,2},{5,4},{6,5},{7,6},{9,8},{10,9},{11,10},{13,12},{... | collective-permute-start | bytes 65288 | tf_op jit(solution)/shard_map/ppermute | solution.py:20
  101.6 0.9 collective-permute-done.10
  102.5 4.1 %collective-permute-done.11 = bf16[10,34,1,32]{3,1,2,0:T(8,128)(2,1)S(1)} collective-permute-done((bf16[10,34,1,32]{3,1,2,0:T(8,128)(2,1)S(1)}, bf16[10,34,1,32]{3,1,2,0:T(8,128)(2,1)S(1)}, u32[]{:S(2)}, u32[]{:S(2)}) %collective-permute-start.11) | collective-permute-done | bytes 21792 | tf_op jit(solution)/shard_map/ppermute | solution.py:20
  106.7 2.1 %maximum_bitcast_fusion = bf16[10,34,1,18,32]{4,1,3,0,2:T(8,128)(2,1)S(1)} fusion(bf16[10,34,1,32]{3,1,2,0:T(8,128)(2,1)S(1)} %collective-permute-done.11, bf16[10,1,16,32]{3,1,2,0:T(2,128)(2,1)S(1)} %collective-permute-done.9, bf16[1,32,16,32]{3,1,2,0:T(8,128)(2,1)S(1)} %collective-permute-done.7, bf16[8,32,16,32]{3,1,2,0:T(8,128)(2,1)S(1)} %fusion.16, ...), kind=kLoop, calls=%fused_computation.19 | loop fusion | flops 2741760 | bytes 783360 | tf_op jit(solution)/shard_map/broadcast_in_dim | solution.py:29
  108.7 2.6 %copy.98 = bf16[10,34,1,18,32]{1,4,3,2,0:T(8,128)(2,1)} copy(bf16[10,34,1,18,32]{4,1,3,0,2:T(8,128)(2,1)S(1)} %maximum_bitcast_fusion) | data formatting | bytes 783360
  111.3 1.8 %pad.2.clone = bf16[10,34,1,24,32]{1,4,3,2,0:T(8,128)(2,1)S(1)} pad(bf16[10,34,1,18,32]{1,4,3,2,0:T(8,128)(2,1)} %copy.98, bf16[]{:T(256)} %constant.34), padding=0_0x0_0x0_0x0_6x0_0 | pad | bytes 913922 | tf_op jit(solution)/shard_map/broadcast_in_dim | solution.py:29
  113.1 3.1 %copy.93 = bf16[10,34,1,8,3,32]{5,3,4,1,0,2:T(8,128)(2,1)} copy(bf16[10,34,1,8,3,32]{1,5,4,3,2,0:T(8,128)(2,1)S(1)} %bitcast.87) | data formatting | bytes 1044480 | tf_op jit(solution)/shard_map/conv_general_dilated | solution.py:28
  116.2 1.9 %slice.87 = bf16[10,34,1,7,2,32]{5,3,4,1,0,2:T(8,128)(2,1)S(1)} slice(bf16[10,34,1,8,3,32]{5,3,4,1,0,2:T(8,128)(2,1)} %copy.93), slice={[0:10], [0:34], [0:1], [1:8], [0:2], [0:32]} | slice | bytes 609280 | tf_op jit(solution)/shard_map/conv_general_dilated | solution.py:28
  118.1 0.1 copy-done.2
  118.2 4.3 %select_convert_fusion = bf16[8,32,8,3,32]{4,2,3,1,0:T(8,128)(2,1)S(1)} fusion(pred[8,3]{0,1:T(4,128)(4,1)S(1)} %copy-done.10, bf16[3,3,3,32,32]{4,3,2,1,0:T(8,128)(2,1)S(1)} %copy-done.7, bf16[10,34,1,7,2,32]{5,3,4,1,0,2:T(8,128)(2,1)S(1)} %slice.87, bf16[10,34,1,8,3,32]{5,3,4,1,0,2:T(8,128)(2,1)S(1)} %copy-done.2), kind=kOutput, calls=%fused_computation.15 | convolution fusion | flops 342743040 | bytes 1275416 | tf_op jit(solution)/shard_map/conv_general_dilated | solution.py:28
  122.6 0.3 copy.94
  123.0 1.4 %copy.95 = bf16[8,32,16,32]{3,2,1,0:T(8,128)(2,1)} copy(bf16[8,32,16,32]{3,1,2,0:T(8,128)(2,1)S(1)} %slice_bitcast_fusion) | data formatting | bytes 524288 | tf_op jit(solution)/shard_map/convert_element_type | solution.py:144
  (54 shorter events, 1.6 us)
Async XLA Ops:
  0.0 53.6 %copy-start = (bf16[256,512]{1,0:T(8,128)(2,1)S(1)}, bf16[256,512]{1,0:T(8,128)(2,1)}, u32[]{:S(2)}) copy-start(bf16[256,512]{1,0:T(8,128)(2,1)} %param.13) | copy-start | bytes 786436
  2.0 7.6 %collective-permute-start = (bf16[1,32,16,32]{1,3,2,0:T(8,128)(2,1)S(1)}, bf16[1,32,16,32]{1,3,2,0:T(8,128)(2,1)S(1)}, u32[]{:S(2)}, u32[]{:S(2)}) collective-permute-start(bf16[1,32,16,32]{1,3,2,0:T(8,128)(2,1)S(1)} %get-tuple-element.36), channel_id=1, source_target_pairs={{0,8},{8,16},{16,24},{1,9},{9,17},{17,25},{2,10},{10,18},{18,26},{... | collective-permute-start | bytes 98312 | tf_op jit(solution)/shard_map/ppermute | solution.py:18
  6.9 7.5 %collective-permute-start.1 = (bf16[1,32,16,32]{1,3,2,0:T(8,128)(2,1)S(1)}, bf16[1,32,16,32]{1,3,2,0:T(8,128)(2,1)S(1)}, u32[]{:S(2)}, u32[]{:S(2)}) collective-permute-start(bf16[1,32,16,32]{1,3,2,0:T(8,128)(2,1)S(1)} %get-tuple-element.37), channel_id=1, source_target_pairs={{8,0},{16,8},{24,16},{9,1},{17,9},{25,17},{10,2},{18,10},{26,18},{... | collective-permute-start | bytes 98312 | tf_op jit(solution)/shard_map/ppermute | solution.py:20
  18.7 3.6 %collective-permute-start.2 = (bf16[10,1,16,32]{3,2,1,0:T(8,128)(2,1)S(1)}, bf16[10,1,16,32]{3,2,1,0:T(8,128)(2,1)S(1)}, u32[]{:S(2)}, u32[]{:S(2)}) collective-permute-start(bf16[10,1,16,32]{3,2,1,0:T(8,128)(2,1)S(1)} %copy.72), channel_id=1, source_target_pairs={{0,4},{1,5},{2,6},{3,7},{8,12},{9,13},{10,14},{11,15},{16,20},{17,... | collective-permute-start | bytes 30728 | tf_op jit(solution)/shard_map/ppermute | solution.py:18
  21.0 3.1 %collective-permute-start.3 = (bf16[10,1,16,32]{3,2,1,0:T(8,128)(2,1)S(1)}, bf16[10,1,16,32]{3,2,1,0:T(8,128)(2,1)S(1)}, u32[]{:S(2)}, u32[]{:S(2)}) collective-permute-start(bf16[10,1,16,32]{3,2,1,0:T(8,128)(2,1)S(1)} %copy.73), channel_id=1, source_target_pairs={{4,0},{5,1},{6,2},{7,3},{12,8},{13,9},{14,10},{15,11},{20,16},{21,... | collective-permute-start | bytes 30728 | tf_op jit(solution)/shard_map/ppermute | solution.py:20
  26.2 11.0 %copy-start.1 = (bf16[10,1,16,32]{1,3,2,0:T(8,128)(2,1)S(1)}, bf16[10,1,16,32]{1,3,2,0:T(8,128)(2,1)}, u32[]{:S(2)}) copy-start(bf16[10,1,16,32]{1,3,2,0:T(8,128)(2,1)} %copy.75) | copy-start | bytes 30724
  27.4 5.7 %collective-permute-start.4 = (bf16[10,34,1,32]{1,3,2,0:T(8,128)(2,1)S(1)}, bf16[10,34,1,32]{1,3,2,0:T(8,128)(2,1)S(1)}, u32[]{:S(2)}, u32[]{:S(2)}) collective-permute-start(bf16[10,34,1,32]{1,3,2,0:T(8,128)(2,1)S(1)} %get-tuple-element.17), channel_id=1, source_target_pairs={{0,1},{1,2},{2,3},{4,5},{5,6},{6,7},{8,9},{9,10},{10,11},{12,13},{... | collective-permute-start | bytes 65288 | tf_op jit(solution)/shard_map/ppermute | solution.py:18
  30.9 6.3 %collective-permute-start.5 = (bf16[10,34,1,32]{1,3,2,0:T(8,128)(2,1)S(1)}, bf16[10,34,1,32]{1,3,2,0:T(8,128)(2,1)S(1)}, u32[]{:S(2)}, u32[]{:S(2)}) collective-permute-start(bf16[10,34,1,32]{1,3,2,0:T(8,128)(2,1)S(1)} %get-tuple-element.18), channel_id=1, source_target_pairs={{1,0},{2,1},{3,2},{5,4},{6,5},{7,6},{9,8},{10,9},{11,10},{13,12},{... | collective-permute-start | bytes 65288 | tf_op jit(solution)/shard_map/ppermute | solution.py:20
  42.0 2.0 %copy-start.3 = (bf16[10,34,1,8,3,32]{5,3,4,1,0,2:T(8,128)(2,1)S(1)}, bf16[10,34,1,8,3,32]{5,3,4,1,0,2:T(8,128)(2,1)}, u32[]{:S(2)}) copy-start(bf16[10,34,1,8,3,32]{5,3,4,1,0,2:T(8,128)(2,1)} %copy.77) | copy-start | bytes 1566724
  42.0 2.0 %copy-start.6 = (bf16[3,3,3,32,32]{4,3,2,1,0:T(8,128)(2,1)S(1)}, bf16[3,3,3,32,32]{4,3,2,1,0:T(8,128)(2,1)}, u32[]{:S(2)}) copy-start(bf16[3,3,3,32,32]{4,3,2,1,0:T(8,128)(2,1)} %param.9) | copy-start | bytes 165892
  42.0 2.0 %copy-start.10 = (pred[8,3]{0,1:T(4,128)(4,1)S(1)}, pred[8,3]{0,1:T(4,128)(4,1)}, u32[]{:S(2)}) copy-start(pred[8,3]{0,1:T(4,128)(4,1)} %constant.42) | copy-start | bytes 76
  48.7 4.7 %copy-start.8 = (bf16[256,256]{1,0:T(8,128)(2,1)S(1)}, bf16[256,256]{1,0:T(8,128)(2,1)}, u32[]{:S(2)}) copy-start(bf16[256,256]{1,0:T(8,128)(2,1)} %param.12) | copy-start | bytes 393220
  48.7 4.7 %copy-start.9 = (f32[256]{0:T(256)S(1)}, f32[256]{0:T(256)}, u32[]{:S(2)}) copy-start(f32[256]{0:T(256)} %param.11) | copy-start | bytes 3076
  50.3 31.9 %copy-start.4 = (bf16[256,256]{1,0:T(8,128)(2,1)S(1)}, bf16[256,256]{1,0:T(8,128)(2,1)}, u32[]{:S(2)}) copy-start(bf16[256,256]{1,0:T(8,128)(2,1)} %param.15) | copy-start | bytes 393220
  50.3 31.9 %copy-start.5 = (bf16[256,256]{1,0:T(8,128)(2,1)S(1)}, bf16[256,256]{1,0:T(8,128)(2,1)}, u32[]{:S(2)}) copy-start(bf16[256,256]{1,0:T(8,128)(2,1)} %param.14) | copy-start | bytes 393220
  83.5 4.7 %collective-permute-start.6 = (bf16[1,32,16,32]{3,1,2,0:T(8,128)(2,1)S(1)}, bf16[1,32,16,32]{3,1,2,0:T(8,128)(2,1)S(1)}, u32[]{:S(2)}, u32[]{:S(2)}) collective-permute-start(bf16[1,32,16,32]{3,1,2,0:T(8,128)(2,1)S(1)} %get-tuple-element.34), channel_id=1, source_target_pairs={{0,8},{8,16},{16,24},{1,9},{9,17},{17,25},{2,10},{10,18},{18,26},{... | collective-permute-start | bytes 98312 | tf_op jit(solution)/shard_map/ppermute | solution.py:18
  85.7 7.2 %collective-permute-start.7 = (bf16[1,32,16,32]{3,1,2,0:T(8,128)(2,1)S(1)}, bf16[1,32,16,32]{3,1,2,0:T(8,128)(2,1)S(1)}, u32[]{:S(2)}, u32[]{:S(2)}) collective-permute-start(bf16[1,32,16,32]{3,1,2,0:T(8,128)(2,1)S(1)} %get-tuple-element.35), channel_id=1, source_target_pairs={{8,0},{16,8},{24,16},{9,1},{17,9},{25,17},{10,2},{18,10},{26,18},{... | collective-permute-start | bytes 98312 | tf_op jit(solution)/shard_map/ppermute | solution.py:20
  93.0 2.6 %collective-permute-start.8 = (bf16[10,1,16,32]{3,1,2,0:T(2,128)(2,1)S(1)}, bf16[10,1,16,32]{3,1,2,0:T(2,128)(2,1)S(1)}, u32[]{:S(2)}, u32[]{:S(2)}) collective-permute-start(bf16[10,1,16,32]{3,1,2,0:T(2,128)(2,1)S(1)} %get-tuple-element.28), channel_id=1, source_target_pairs={{0,4},{1,5},{2,6},{3,7},{8,12},{9,13},{10,14},{11,15},{16,20},{17,... | collective-permute-start | bytes 30728 | tf_op jit(solution)/shard_map/ppermute | solution.py:18
  94.3 3.2 %collective-permute-start.9 = (bf16[10,1,16,32]{3,1,2,0:T(2,128)(2,1)S(1)}, bf16[10,1,16,32]{3,1,2,0:T(2,128)(2,1)S(1)}, u32[]{:S(2)}, u32[]{:S(2)}) collective-permute-start(bf16[10,1,16,32]{3,1,2,0:T(2,128)(2,1)S(1)} %get-tuple-element.30), channel_id=1, source_target_pairs={{4,0},{5,1},{6,2},{7,3},{12,8},{13,9},{14,10},{15,11},{20,16},{21,... | collective-permute-start | bytes 30728 | tf_op jit(solution)/shard_map/ppermute | solution.py:20
  97.6 4.9 %collective-permute-start.10 = (bf16[10,34,1,32]{3,1,2,0:T(8,128)(2,1)S(1)}, bf16[10,34,1,32]{3,1,2,0:T(8,128)(2,1)S(1)}, u32[]{:S(2)}, u32[]{:S(2)}) collective-permute-start(bf16[10,34,1,32]{3,1,2,0:T(8,128)(2,1)S(1)} %get-tuple-element.19), channel_id=1, source_target_pairs={{0,1},{1,2},{2,3},{4,5},{5,6},{6,7},{8,9},{9,10},{10,11},{12,13},{... | collective-permute-start | bytes 65288 | tf_op jit(solution)/shard_map/ppermute | solution.py:18
  100.1 6.6 %collective-permute-start.11 = (bf16[10,34,1,32]{3,1,2,0:T(8,128)(2,1)S(1)}, bf16[10,34,1,32]{3,1,2,0:T(8,128)(2,1)S(1)}, u32[]{:S(2)}, u32[]{:S(2)}) collective-permute-start(bf16[10,34,1,32]{3,1,2,0:T(8,128)(2,1)S(1)} %get-tuple-element.20), channel_id=1, source_target_pairs={{1,0},{2,1},{3,2},{5,4},{6,5},{7,6},{9,8},{10,9},{11,10},{13,12},{... | collective-permute-start | bytes 65288 | tf_op jit(solution)/shard_map/ppermute | solution.py:20
  116.2 2.0 %copy-start.2 = (bf16[10,34,1,8,3,32]{5,3,4,1,0,2:T(8,128)(2,1)S(1)}, bf16[10,34,1,8,3,32]{5,3,4,1,0,2:T(8,128)(2,1)}, u32[]{:S(2)}) copy-start(bf16[10,34,1,8,3,32]{5,3,4,1,0,2:T(8,128)(2,1)} %copy.93) | copy-start | bytes 1566724
  116.2 2.0 %copy-start.7 = (bf16[3,3,3,32,32]{4,3,2,1,0:T(8,128)(2,1)S(1)}, bf16[3,3,3,32,32]{4,3,2,1,0:T(8,128)(2,1)}, u32[]{:S(2)}) copy-start(bf16[3,3,3,32,32]{4,3,2,1,0:T(8,128)(2,1)} %param.10) | copy-start | bytes 165892
